TPU v7x, 512 devices: a whole 4x4x16 slice. The times are simulated.
512 devices in a mesh: rows: 16 (over y, z_lo), cols: 32 (over z_hi, x, core).
Axes of the slice: x: 4, y: 4, z: 16 (z_hi: 4, z_lo: 4; z = z_hi * 4 + z_lo), core: 2. Of those that a mesh axis runs over, the one named last changes fastest.
Arguments:
- factor_u: float32 [16, 8192, 128], P('rows', 'cols'), may hold values from -2 to 2
- factor_v: float32 [32, 2048, 128], P('cols', 'rows'), may hold values from -2 to 2
- values: bfloat16 [16, 32, 32, 256, 256], P('rows', 'cols'), may hold values from -6 to 6
- mask_words: int32 [16, 32, 32, 16, 256], P('rows', 'cols'), may hold values from 0 to 65535, as said below
- tile_cols: int32 [16, 32, 32], P('rows', 'cols'), may hold values from 0 to 7
Outputs:
- new_u: float32 [16, 8192, 128], P('rows', 'cols')
- new_v: float32 [32, 2048, 128], P('cols', 'rows')
- loss: float32 [], replicated
Inputs may be any that keep to these rules, and one draw needn't show every extreme that they name: `mask_words`: bit b of word w of a slot marks the entry in row 16 w + b of the tile.
All inputs are finite; a program needn't handle non-finite values.
Results may differ from a plain program's by a relative error of at most 0.02.
Values may be sent and summed in bfloat16 or wider, within the bound.
A program may use at most 64 MiB of HBM per device.

v0:
```python
import jax
import jax.numpy as jnp
from jax import lax
from jax.sharding import Mesh
from jax.sharding import PartitionSpec as P

ROWS = ("rows_0", "rows_1")
COLS = ("cols_0", "cols_1", "cols_2")
ROWS_COLS = ("rows_0", "rows_1", "cols_0", "cols_1", "cols_2")
step_rate = 0.01
ridge_weight = 0.1


def from_everyone(array, axis):
    copies = jnp.broadcast_to(array, (lax.axis_size(axis), *array.shape))
    return lax.all_to_all(copies, axis, split_axis=0, concat_axis=0, tiled=True)


def laid_out(tiles, dim):
    tiles = jnp.moveaxis(tiles, 0, dim)
    dims = tiles.shape
    return tiles.reshape(*dims[:dim], dims[dim] * dims[dim + 1], *dims[dim + 2 :])


def gathered_copies(array, axis, dim):
    tiles = from_everyone(array, axis)
    return laid_out(tiles, dim)


def in_blocks(array, dim, count):
    dims = array.shape
    tiles = array.reshape(*dims[:dim], count, dims[dim] // count, *dims[dim + 1 :])
    return jnp.moveaxis(tiles, dim, 0)


def sum_by_chip(array, chips, core, dim):
    sizes = (lax.axis_size(chips), lax.axis_size(core))
    tiles = in_blocks(array, dim, sizes[0] * sizes[1])
    inside = tiles.shape[1:]
    tiles = tiles.reshape(*sizes, *inside).swapaxes(0, 1).reshape(-1, *inside)
    tiles = lax.psum_scatter(tiles, core, scatter_dimension=0, tiled=True)
    return lax.psum_scatter(tiles, chips, scatter_dimension=0, tiled=True)[0]


def summed_on_arrival(array, axis, dim):
    count = lax.axis_size(axis)
    tiles = lax.all_to_all(in_blocks(array, dim, count), axis, 0, 0, tiled=True)
    return jnp.sum(tiles.astype(jnp.float32), axis=0)


def by_axis(array, axes):
    for axis in axes:
        array = lax.psum(array, axis)
    return array


def decode(mask_bits):
    shifts = jnp.arange(16, dtype=jnp.int32)
    bit_values = jnp.bitwise_and(
        jnp.right_shift(mask_bits[:, :, None, :], shifts[None, None, :, None]), 1
    )
    return bit_values.reshape(
        mask_bits.shape[0], mask_bits.shape[1] * 16, mask_bits.shape[2]
    ).astype(jnp.float32)


def slot_terms(left_rows, tile_values, mask_bits, column_ids, right_tiles):
    observed = decode(mask_bits)
    right_rows = jnp.take(right_tiles, column_ids, axis=0)
    predicted = jnp.einsum(
        "sik,sjk->sij", left_rows, right_rows, preferred_element_type=jnp.float32
    )
    residual = observed * (predicted - tile_values.astype(jnp.float32))
    squares = 0.5 * jnp.sum(residual * residual)
    resid_low = residual.astype(jnp.bfloat16)
    grad_rows = jnp.einsum(
        "sij,sjk->sik", resid_low, right_rows, preferred_element_type=jnp.float32
    )
    first = grad_rows.reshape(-1, left_rows.shape[2])
    grad_cols = jnp.einsum("sij,sik->sjk", resid_low, left_rows, preferred_element_type=jnp.float32)
    selector = (
        column_ids[:, None] == jnp.arange(right_tiles.shape[0], dtype=jnp.int32)[None, :]
    ).astype(jnp.float32)
    col_sums = jnp.einsum(
        "sq,sx->qx",
        selector,
        grad_cols.reshape(grad_cols.shape[0], -1),
        precision=lax.Precision.HIGHEST,
        preferred_element_type=jnp.float32,
    )
    return (first, col_sums, squares)


def band_terms(left_tiles, tile_values, mask_bits, column_ids, right_tiles):
    tile_count = left_tiles.shape[0]
    row_parts = []
    col_total = jnp.zeros(
        (right_tiles.shape[0], right_tiles.shape[1] * right_tiles.shape[2]), jnp.float32
    )
    square_total = jnp.zeros((), jnp.float32)
    for block_start in range(0, tile_count, 8):
        block_len = min(8, tile_count - block_start)
        block_end = block_start + block_len
        first, col_sums, squares = slot_terms(
            left_tiles[block_start:block_end],
            tile_values[block_start:block_end],
            mask_bits[block_start:block_end],
            column_ids[block_start:block_end],
            right_tiles,
        )
        row_parts.append(first)
        col_total = col_total + col_sums
        square_total = square_total + squares
    return (jnp.concatenate(row_parts, axis=0), col_total, square_total)


def per_device(factor_u, factor_v, values, mask_words, tile_cols):
    owned_left = factor_u[0]
    owned_right = factor_v[0]
    tile_values = values[0, 0]
    mask_bits = mask_words[0, 0]
    column_ids = tile_cols[0, 0]
    tile_size = tile_values.shape[-1]
    factor_rank = owned_left.shape[-1]
    slot_count = tile_values.shape[0]
    v_band = gathered_copies(owned_right.astype(jnp.bfloat16), ROWS, 0)
    right_tiles = v_band.reshape(-1, tile_size, factor_rank)
    u_low = owned_left.astype(jnp.bfloat16)
    u_band = lax.all_gather(u_low, COLS, axis=0, tiled=True)
    first_rows, col_total, square_total = band_terms(
        u_band.reshape(-1, tile_size, factor_rank), tile_values, mask_bits, column_ids, right_tiles
    )
    grad_u = sum_by_chip(first_rows.astype(jnp.bfloat16), ("cols_0", "cols_1"), "cols_2", 0).astype(
        jnp.float32
    )
    grad_v = summed_on_arrival(col_total.reshape(-1, factor_rank).astype(jnp.bfloat16), ROWS, 0)
    local_sum = square_total + 0.5 * ridge_weight * (
        jnp.sum(owned_left * owned_left) + jnp.sum(owned_right * owned_right)
    )
    total = by_axis(local_sum, ROWS_COLS)
    entries = lax.axis_size(ROWS) * lax.axis_size(COLS) * slot_count * tile_size * tile_size
    new_left = owned_left - step_rate * (grad_u + ridge_weight * owned_left)
    new_right = owned_right - step_rate * (grad_v + ridge_weight * owned_right)
    return (new_left[None], new_right[None], total / entries)


def solution(mesh):
    split = Mesh(
        mesh.devices.reshape(4, 4, 4, 4, 2), ("rows_0", "rows_1", "cols_0", "cols_1", "cols_2")
    )
    in_specs = (
        P(ROWS, COLS, None),
        P(COLS, ROWS, None),
        P(ROWS, COLS, None, None, None),
        P(ROWS, COLS, None, None, None),
        P(ROWS, COLS, None),
    )
    out_specs = (P(ROWS, COLS, None), P(COLS, ROWS, None), P())
    return jax.shard_map(
        per_device, mesh=split, in_specs=in_specs, out_specs=out_specs, check_vma=False
    )
```

profile of v0, /device:TPU:8, one launch (start us, length us, event | category | flops | bytes accessed | tf_op | source)
XLA Modules:
  0.0 256.3 jit_solution(2091023990044940334)
XLA Ops:
  7.2 2.2 multiply_reduce_fusion.4
  9.5 1.5 multiply_reduce_fusion.5
  11.0 0.9 broadcast_in_dim.11
  11.9 9.2 %all-to-all-start = ((bf16[16,128,128]{2,1,0:T(8,128)(2,1)}), bf16[16,128,128]{2,1,0:T(8,128)(2,1)S(1)}, u32[]{:S(2)}, u32[]{:S(2)}) async-start(bf16[16,128,128]{2,1,0:T(8,128)(2,1)} %broadcast_in_dim.11), calls=%async_computation | async-start | bytes 1048576 | tf_op jit(solution)/shard_map/all_to_all | solution.py:16
  21.1 3.9 %fusion.36 = (bf16[1,1,8,256,256]{4,3,2,1,0:T(8,128)(2,1)}, bf16[1,1,8,256,256]{4,3,2,1,0:T(8,128)(2,1)}, bf16[1,1,8,256,256]{4,3,2,1,0:T(8,128)(2,1)}, bf16[1,1,8,256,256]{4,3,2,1,0:T(8,128)(2,1)S(1)}) fusion(bf16[1,1,32,256,256]{4,3,2,1,0:T(8,128)(2,1)} %param.9), kind=kLoop, calls=%fused_computation.94 | loop fusion | bytes 8388608 | tf_op jit(solution)/shard_map/slice | solution.py:106
  25.0 1.3 copy.41
  26.4 1.5 shift_right_arithmetic.104
  27.9 1.9 copy.30
  29.9 2.2 copy.40
  32.2 1.6 shift_right_arithmetic.100
  33.7 2.9 %copy.27 = s32[8,256,256]{1,2,0:T(8,128)} copy(s32[8,256,256]{2,1,0:T(8,128)} %bitcast.116) | data formatting | bytes 4194304 | tf_op jit(solution)/shard_map/shift_right_arithmetic | solution.py:60
  36.7 2.3 copy.39
  38.9 1.5 shift_right_arithmetic.96
  40.4 2.9 %copy.24 = s32[8,256,256]{1,2,0:T(8,128)} copy(s32[8,256,256]{2,1,0:T(8,128)} %bitcast.117) | data formatting | bytes 4194304 | tf_op jit(solution)/shard_map/shift_right_arithmetic | solution.py:60
  43.3 2.3 copy.38
  45.6 1.5 shift_right_arithmetic.89
  47.1 2.9 %copy.21 = s32[8,256,256]{1,2,0:T(8,128)} copy(s32[8,256,256]{2,1,0:T(8,128)} %bitcast.118) | data formatting | bytes 4194304 | tf_op jit(solution)/shard_map/shift_right_arithmetic | solution.py:60
  50.1 1.4 gather_fusion.3
  51.5 1.4 gather_fusion.2
  52.9 1.4 gather_fusion.1
  54.3 1.4 gather_fusion
  55.8 38.8 %all-gather.3.cloned.1.call-done = bf16[1,8192,128]{2,1,0:T(8,128)(2,1)} async-done(((bf16[1,256,128]{2,1,0:T(8,128)(2,1)}), bf16[1,8192,128]{2,1,0:T(8,128)(2,1)}) %all-gather.3.cloned.1.call-update) | async-done | bytes 2097168 | tf_op jit(solution)/shard_map/all_gather | solution.py:129
  94.6 1.8 fusion.37
  96.4 0.8 copy-done.8
  97.2 1.5 multiply_reduce_fusion
  99.2 1.0 copy-done.3
  100.3 1.5 multiply_reduce_fusion.1
  102.3 1.0 copy-done.2
  103.3 1.5 multiply_reduce_fusion.2
  105.4 1.0 copy-done.1
  106.5 1.5 multiply_reduce_fusion.3
  108.0 1.0 copy-done
  109.6 1.6 copy.33
  111.3 1.8 convolution_bitcast_fusion.3
  114.7 1.2 fusion.11
  115.9 1.2 convolution_add_fusion.2
  117.1 1.2 convolution_add_fusion.1
  118.4 1.3 fusion
  119.7 1.0 convert_element_type.106
  120.7 5.2 %all-to-all-start.1 = ((bf16[16,128,128]{2,1,0:T(8,128)(2,1)}), bf16[16,128,128]{2,1,0:T(8,128)(2,1)S(1)}, u32[]{:S(2)}, u32[]{:S(2)}) async-start(bf16[16,128,128]{2,1,0:T(8,128)(2,1)} %convert_element_type.106), calls=%async_computation.3 | async-start | bytes 1048576 | tf_op jit(solution)/shard_map/all_to_all | solution.py:47
  130.4 9.2 %psum.35 = f32[]{:T(128)} all-reduce(f32[]{:T(128)S(6)} %add.61), channel_id=1, replica_groups=mesh['rows_0'=4,'rows_1'=4,'cols_0'=4,'cols_1'=4,'cols_2'=2] {'rows_0'}, use_global_device_ids=true, to_apply=%region_9.11 | all-reduce | flops 1 | bytes 8 | tf_op jit(solution)/shard_map/psum | solution.py:53
  139.6 12.2 %psum.36 = f32[]{:T(128)} all-reduce(f32[]{:T(128)} %psum.35), channel_id=1, replica_groups=mesh['rows_0'=4,'rows_1'=4,'cols_0'=4,'cols_1'=4,'cols_2'=2] {'rows_1'}, use_global_device_ids=true, to_apply=%region_10.12 | all-reduce | flops 1 | bytes 8 | tf_op jit(solution)/shard_map/psum | solution.py:53
  151.8 16.5 %psum.37 = f32[]{:T(128)} all-reduce(f32[]{:T(128)} %psum.36), channel_id=1, replica_groups=mesh['rows_0'=4,'rows_1'=4,'cols_0'=4,'cols_1'=4,'cols_2'=2] {'cols_0'}, use_global_device_ids=true, to_apply=%region_11.13 | all-reduce | flops 1 | bytes 8 | tf_op jit(solution)/shard_map/psum | solution.py:53
  168.3 11.0 %psum.38 = f32[]{:T(128)} all-reduce(f32[]{:T(128)} %psum.37), channel_id=1, replica_groups=mesh['rows_0'=4,'rows_1'=4,'cols_0'=4,'cols_1'=4,'cols_2'=2] {'cols_1'}, use_global_device_ids=true, to_apply=%region_12.14 | all-reduce | flops 1 | bytes 8 | tf_op jit(solution)/shard_map/psum | solution.py:53
  179.3 3.1 %psum.39 = f32[]{:T(128)} all-reduce(f32[]{:T(128)} %psum.38), channel_id=1, replica_groups=mesh['rows_0'=4,'rows_1'=4,'cols_0'=4,'cols_1'=4,'cols_2'=2] {'cols_2'}, use_global_device_ids=true, to_apply=%region_13.15 | all-reduce | flops 1 | bytes 8 | tf_op jit(solution)/shard_map/psum | solution.py:53
  183.1 0.6 fusion.23
  183.8 63.4 %reduce-scatter.5.cloned.1.call-done = bf16[1,256,128]{2,1,0:T(8,128)(2,1)} async-done(((bf16[16,256,128]{2,1,0:T(8,128)(2,1)}), bf16[1,256,128]{2,1,0:T(8,128)(2,1)}) %reduce-scatter.5.cloned.1.call-update) | async-done | bytes 65552 | tf_op jit(solution)/shard_map/reduce_scatter | solution.py:42
  247.1 1.5 multiply_subtract_fusion
  (66 shorter events, 4.9 us)
Async XLA Ops:
  7.2 87.5 %all-gather.3.cloned.1.call-start = ((), (), s32[]{:S(2)}) async-start(), calls=%async_computation.6 | async-start | bytes 2162688 | tf_op jit(solution)/shard_map/all_gather | solution.py:129
  11.9 38.2 %all-to-all-start = ((bf16[16,128,128]{2,1,0:T(8,128)(2,1)}), bf16[16,128,128]{2,1,0:T(8,128)(2,1)S(1)}, u32[]{:S(2)}, u32[]{:S(2)}) async-start(bf16[16,128,128]{2,1,0:T(8,128)(2,1)} %broadcast_in_dim.11), calls=%async_computation | async-start | bytes 1048576 | tf_op jit(solution)/shard_map/all_to_all | solution.py:16
  21.1 104.9 %reduce-scatter.3.cloned.1.call-start = ((), (), s32[]{:S(2)}) async-start(), calls=%async_computation.4 | async-start | bytes 3145728 | tf_op jit(solution)/shard_map/reduce_scatter | solution.py:41
  25.0 1.3 copy-start.19
  47.1 2.9 %copy-start.22 = (s32[1,1,32]{2,1,0:T(1,128)S(1)}, s32[1,1,32]{2,1,0:T(1,128)}, u32[]{:S(2)}) copy-start(s32[1,1,32]{2,1,0:T(1,128)} %param.11) | copy-start | bytes 388
  94.6 2.6 %copy-start.7 = (bf16[8,256,128]{2,1,0:T(8,128)(2,1)S(1)}, bf16[8,256,128]{2,1,0:T(8,128)(2,1)}, u32[]{:S(2)}) copy-start(bf16[8,256,128]{2,1,0:T(8,128)(2,1)} %gather_fusion.3) | copy-start | bytes 1572868
  94.6 2.6 %copy-start.15 = (bf16[1,1,8,256,256]{3,4,2,1,0:T(8,128)(2,1)S(1)}, bf16[1,1,8,256,256]{3,4,2,1,0:T(8,128)(2,1)}, u32[]{:S(2)}) copy-start(bf16[1,1,8,256,256]{3,4,2,1,0:T(8,128)(2,1)} %copy.41) | copy-start | bytes 3145732
  96.4 0.8 copy-start.8
  96.4 2.8 %copy-start.10 = (bf16[1,2048,128]{2,1,0:T(8,128)(2,1)}, bf16[1,2048,128]{2,1,0:T(8,128)(2,1)S(1)}, u32[]{:S(2)}) copy-start(bf16[1,2048,128]{2,1,0:T(8,128)(2,1)S(1)} %get-tuple-element.17) | copy-start | bytes 1572868
  96.4 5.9 %copy-start.12 = (bf16[1,2048,128]{2,1,0:T(8,128)(2,1)}, bf16[1,2048,128]{2,1,0:T(8,128)(2,1)S(1)}, u32[]{:S(2)}) copy-start(bf16[1,2048,128]{2,1,0:T(8,128)(2,1)S(1)} %get-tuple-element.18) | copy-start | bytes 1572868
  96.4 9.0 %copy-start.14 = (bf16[1,2048,128]{2,1,0:T(8,128)(2,1)}, bf16[1,2048,128]{2,1,0:T(8,128)(2,1)S(1)}, u32[]{:S(2)}) copy-start(bf16[1,2048,128]{2,1,0:T(8,128)(2,1)S(1)} %get-tuple-element.16) | copy-start | bytes 1572868
  97.2 2.0 copy-start.6
  97.2 2.0 copy-start.18
  98.7 1.6 copy-start.3
  100.3 2.0 copy-start.5
  100.3 2.0 copy-start.17
  101.7 1.6 copy-start.2
  103.3 2.1 copy-start.4
  103.3 2.1 copy-start.16
  104.9 1.6 copy-start.1
  108.0 1.0 copy-start
  111.2 1.9 copy-start.13
  111.3 2.3 copy-start.11
  113.2 1.0 copy-start.9
  119.6 63.5 %copy-start.21 = (f32[1,128,128]{2,1,0:T(8,128)S(1)}, f32[1,128,128]{2,1,0:T(8,128)}, u32[]{:S(2)}) copy-start(f32[1,128,128]{2,1,0:T(8,128)} %param.8) | copy-start | bytes 196612
  119.7 127.5 %copy-start.20 = (f32[1,256,128]{2,1,0:T(8,128)S(1)}, f32[1,256,128]{2,1,0:T(8,128)}, u32[]{:S(2)}) copy-start(f32[1,256,128]{2,1,0:T(8,128)} %param.7) | copy-start | bytes 393220
  120.7 62.3 %all-to-all-start.1 = ((bf16[16,128,128]{2,1,0:T(8,128)(2,1)}), bf16[16,128,128]{2,1,0:T(8,128)(2,1)S(1)}, u32[]{:S(2)}, u32[]{:S(2)}) async-start(bf16[16,128,128]{2,1,0:T(8,128)(2,1)} %convert_element_type.106), calls=%async_computation.3 | async-start | bytes 1048576 | tf_op jit(solution)/shard_map/all_to_all | solution.py:47
  125.9 121.2 %reduce-scatter.5.cloned.1.call-start = ((), (), s32[]{:S(2)}) async-start(), calls=%async_computation.5 | async-start | bytes 1114112 | tf_op jit(solution)/shard_map/reduce_scatter | solution.py:42
Sparse Core Ops, SparseCore 0:
  11.7 82.8 all-gather.2
  111.3 14.6 reduce-scatter.2
  130.8 116.3 reduce-scatter.4
where the time goes:
time: 257 us; the launch traced here: 256 us
  waiting for transfers between devices  103 us (40%)
  blocking collectives  51.9 us (20%)
  local copies, waits for them, and re-layouts  45 us (18%)
  between operations  19.7 us (8%)
  matrix products  16.1 us (6%)
  starting transfers between devices  14.5 us (6%)
  other arithmetic  6.22 us (2%)
    reduce_scatter x1, waiting for transfers between devices, sum_by_chip(): return lax.psum_scatter(tiles, chips, scatter_dimension=0, tiled=True)[0]  63.4 us
    psum x5, blocking collectives, by_axis(): array = lax.psum(array, axis)  51.9 us
    all_gather x1, waiting for transfers between devices, per_device(): u_band = lax.all_gather(u_low, COLS, axis=0, tiled=True)  38.8 us
    shift_right_arithmetic x11, local copies, waits for them, and re-layouts, decode(): jnp.right_shift(mask_bits[:, :, None, :], shifts[None, None, :, None])  16.8 us
    unnamed x50, local copies, waits for them, and re-layouts  13.2 us
    all_to_all x1, starting transfers between devices, from_everyone(): return lax.all_to_all(copies, axis, split_axis=0, concat_axis=0, tiled=True)  9.17 us
    dot_general x4, matrix products, slot_terms(): jnp.einsum('sik,sjk->sij', left_rows, right_rows, preferred_element_type=...  5.97 us
    gather x4, local copies, waits for them, and re-layouts, slot_terms(): right_rows = jnp.take(right_tiles, column_ids, axis=0)  5.66 us
  transfers between devices with their start and end apart: 5, of which 3 were waited for; matrix products, arithmetic and copies ran while one was open for 18% of the time, Pallas kernels for 0%

commit v1 on v0

--- a/solution.py
+++ b/solution.py
@@ -126,7 +126,10 @@
     v_band = gathered_copies(owned_right.astype(jnp.bfloat16), ROWS, 0)
     right_tiles = v_band.reshape(-1, tile_size, factor_rank)
     u_low = owned_left.astype(jnp.bfloat16)
-    u_band = lax.all_gather(u_low, COLS, axis=0, tiled=True)
+    devices = lax.axis_size(COLS)
+    tiles_2 = jnp.stack([u_low for _ in range(devices)])
+    tiles_2 = lax.all_to_all(tiles_2, COLS, split_axis=0, concat_axis=0)
+    u_band = jnp.concatenate(tiles_2, axis=0)
     first_rows, col_total, square_total = band_terms(
         u_band.reshape(-1, tile_size, factor_rank), tile_values, mask_bits, column_ids, right_tiles
     )

time: 257 us -> 310 us (1.21)
  waiting for transfers between devices: 103 us -> 138 us
  starting transfers between devices: 14.5 us -> 32 us
    all_to_all x0 -> x1, waiting for transfers between devices: none -> 61.9 us  [per_device(): tiles_2 = lax.all_to_all(tiles_2, COLS, split_axis=0, concat_axis=0)]
    all_gather x1 -> x0, waiting for transfers between devices: 38.8 us -> none  [per_device(): u_band = lax.all_gather(u_low, COLS, axis=0, tiled=True)]
    all_to_all x0 -> x1, starting transfers between devices: none -> 15.2 us  [per_device(): tiles_2 = lax.all_to_all(tiles_2, COLS, split_axis=0, concat_axis=0)]
    all_to_all x1, waiting for transfers between devices: 0.01 us -> 12.1 us  [from_everyone(): return lax.all_to_all(copies, axis, split_axis=0, concat_axis=0, tiled=True)]
    unnamed x50 -> x42, local copies, waits for them, and re-layouts: 13.2 us -> 13 us
  transfers between devices with their start and end apart: 5 -> 5, of which waited for: 3 -> 3; matrix products, arithmetic and copies ran while one was open for 18% -> 16% of each run, Pallas kernels for 0% -> 0%
where the time goes in v1:
time: 310 us; the launch traced here: 309 us
  waiting for transfers between devices  138 us (45%)
  blocking collectives  49.5 us (16%)
  local copies, waits for them, and re-layouts  46.1 us (15%)
  starting transfers between devices  32 us (10%)
  between operations  19.9 us (6%)
  matrix products  18.2 us (6%)
  other arithmetic  5.62 us (2%)
    reduce_scatter x1, waiting for transfers between devices, sum_by_chip(): return lax.psum_scatter(tiles, chips, scatter_dimension=0, tiled=True)[0]  63.4 us
    all_to_all x1, waiting for transfers between devices, per_device(): tiles_2 = lax.all_to_all(tiles_2, COLS, split_axis=0, concat_axis=0)  61.9 us
    psum x5, blocking collectives, by_axis(): array = lax.psum(array, axis)  49.5 us
    shift_right_arithmetic x11, local copies, waits for them, and re-layouts, decode(): jnp.right_shift(mask_bits[:, :, None, :], shifts[None, None, :, None])  17.8 us
    all_to_all x1, starting transfers between devices, per_device(): tiles_2 = lax.all_to_all(tiles_2, COLS, split_axis=0, concat_axis=0)  15.2 us
    unnamed x42, local copies, waits for them, and re-layouts  13 us
    all_to_all x1, waiting for transfers between devices, from_everyone(): return lax.all_to_all(copies, axis, split_axis=0, concat_axis=0, tiled=True)  12.1 us
    all_to_all x1, starting transfers between devices, from_everyone(): return lax.all_to_all(copies, axis, split_axis=0, concat_axis=0, tiled=True)  9.17 us
  transfers between devices with their start and end apart: 5, of which 3 were waited for; matrix products, arithmetic and copies ran while one was open for 16% of the time, Pallas kernels for 0%

profile of v1, /device:TPU:8, one launch (start us, length us, event | category | flops | bytes accessed | tf_op | source)
XLA Modules:
  0.0 309.4 jit_solution(4806306272726124063)
XLA Ops:
  7.2 1.5 multiply_reduce_fusion.5
  8.7 0.9 broadcast_in_dim.11
  9.6 9.2 %all-to-all-start = ((bf16[16,128,128]{2,1,0:T(8,128)(2,1)}), bf16[16,128,128]{2,1,0:T(8,128)(2,1)S(1)}, u32[]{:S(2)}, u32[]{:S(2)}) async-start(bf16[16,128,128]{2,1,0:T(8,128)(2,1)} %broadcast_in_dim.11), calls=%async_computation | async-start | bytes 1048576 | tf_op jit(solution)/shard_map/all_to_all | solution.py:16
  18.8 1.6 multiply_reduce_fusion.4
  20.4 12.1 %all-to-all-done = bf16[16,128,128]{2,1,0:T(8,128)(2,1)S(1)} async-done(((bf16[16,128,128]{2,1,0:T(8,128)(2,1)}), bf16[16,128,128]{2,1,0:T(8,128)(2,1)S(1)}, u32[]{:S(2)}, u32[]{:S(2)}) %all-to-all-start) | async-done | bytes 524320 | tf_op jit(solution)/shard_map/all_to_all | solution.py:16
  32.5 1.8 stack.5
  34.3 15.2 %all-to-all-start.1 = ((bf16[32,256,128]{2,1,0:T(8,128)(2,1)}), bf16[32,256,128]{2,1,0:T(8,128)(2,1)S(1)}, u32[]{:S(2)}, u32[]{:S(2)}) async-start(bf16[32,256,128]{2,1,0:T(8,128)(2,1)} %stack.5), calls=%async_computation.1 | async-start | bytes 4194304 | tf_op jit(solution)/shard_map/all_to_all | solution.py:131
  49.6 4.3 %fusion.44 = (bf16[1,1,8,256,256]{4,3,2,1,0:T(8,128)(2,1)}, bf16[1,1,8,256,256]{4,3,2,1,0:T(8,128)(2,1)}, bf16[1,1,8,256,256]{4,3,2,1,0:T(8,128)(2,1)}, bf16[1,1,8,256,256]{4,3,2,1,0:T(8,128)(2,1)}) fusion(bf16[1,1,32,256,256]{4,3,2,1,0:T(8,128)(2,1)} %param.9), kind=kLoop, calls=%fused_computation.103 | loop fusion | bytes 8388608 | tf_op jit(solution)/shard_map/slice | solution.py:106
  53.9 2.4 copy.41
  56.3 1.5 shift_right_arithmetic.104
  57.8 2.9 copy.30
  60.7 2.3 copy.40
  63.0 1.5 shift_right_arithmetic.100
  64.5 2.9 copy.27
  67.4 2.3 copy.39
  69.7 1.5 shift_right_arithmetic.96
  71.2 2.9 copy.24
  74.1 2.3 copy.38
  76.4 1.5 shift_right_arithmetic.89
  77.9 2.9 copy.21
  80.9 1.4 gather_fusion.3
  82.4 1.4 gather_fusion.2
  83.8 1.4 gather_fusion.1
  85.2 1.4 gather_fusion
  86.6 61.9 %all-to-all-done.1 = bf16[32,256,128]{2,1,0:T(8,128)(2,1)S(1)} async-done(((bf16[32,256,128]{2,1,0:T(8,128)(2,1)}), bf16[32,256,128]{2,1,0:T(8,128)(2,1)S(1)}, u32[]{:S(2)}, u32[]{:S(2)}) %all-to-all-start.1) | async-done | bytes 2097184 | tf_op jit(solution)/shard_map/all_to_all | solution.py:131
  148.5 3.6 %multiply_reduce_fusion = (f32[]{:T(128)}, bf16[8,256,256]{1,2,0:T(8,128)(2,1)S(1)}) fusion(bf16[1,1,8,256,256]{3,4,2,1,0:T(8,128)(2,1)} %copy.41, bf16[32,256,128]{2,1,0:T(8,128)(2,1)S(1)} %all-to-all-done.1, bf16[8,256,128]{2,1,0:T(8,128)(2,1)} %gather_fusion.3, pred[8]{0:T(512)(128)(4,1)S(1)} %get-tuple-element.28, s32[8,256,256]{1,2,0:T(8,128)} %copy.30, ...), kind=kOutput, calls=%fused_computation.17 | convolution fusion | flops 139198464 | bytes 5244420 | tf_op jit(solution)/shard_map/sik,sjk->sij/dot_general | solution.py:70
  153.5 1.5 multiply_reduce_fusion.1
  155.6 0.9 copy-done.6
  156.8 1.5 multiply_reduce_fusion.2
  158.9 0.9 copy-done.5
  160.1 1.5 multiply_reduce_fusion.3
  162.7 1.6 copy.33
  164.4 1.8 convolution_bitcast_fusion.3
  167.5 1.2 fusion.11
  168.8 1.2 convolution_add_fusion.2
  170.0 1.2 convolution_add_fusion.1
  171.2 1.3 fusion
  172.5 1.0 convert_element_type.103
  173.6 7.5 %all-to-all-start.2 = ((bf16[16,128,128]{2,1,0:T(8,128)(2,1)}), bf16[16,128,128]{2,1,0:T(8,128)(2,1)S(1)}, u32[]{:S(2)}, u32[]{:S(2)}) async-start(bf16[16,128,128]{2,1,0:T(8,128)(2,1)} %convert_element_type.103), calls=%async_computation.4 | async-start | bytes 1048576 | tf_op jit(solution)/shard_map/all_to_all | solution.py:47
  181.1 0.7 reduce-scatter.5.cloned.1.call-update
  185.7 9.1 %psum.35 = f32[]{:T(128)} all-reduce(f32[]{:T(128)S(6)} %add.61), channel_id=1, replica_groups=mesh['rows_0'=4,'rows_1'=4,'cols_0'=4,'cols_1'=4,'cols_2'=2] {'rows_0'}, use_global_device_ids=true, to_apply=%region_9.11 | all-reduce | flops 1 | bytes 8 | tf_op jit(solution)/shard_map/psum | solution.py:53
  194.8 12.2 %psum.36 = f32[]{:T(128)} all-reduce(f32[]{:T(128)} %psum.35), channel_id=1, replica_groups=mesh['rows_0'=4,'rows_1'=4,'cols_0'=4,'cols_1'=4,'cols_2'=2] {'rows_1'}, use_global_device_ids=true, to_apply=%region_10.12 | all-reduce | flops 1 | bytes 8 | tf_op jit(solution)/shard_map/psum | solution.py:53
  207.0 14.2 %psum.37 = f32[]{:T(128)} all-reduce(f32[]{:T(128)} %psum.36), channel_id=1, replica_groups=mesh['rows_0'=4,'rows_1'=4,'cols_0'=4,'cols_1'=4,'cols_2'=2] {'cols_0'}, use_global_device_ids=true, to_apply=%region_11.13 | all-reduce | flops 1 | bytes 8 | tf_op jit(solution)/shard_map/psum | solution.py:53
  221.3 10.8 %psum.38 = f32[]{:T(128)} all-reduce(f32[]{:T(128)} %psum.37), channel_id=1, replica_groups=mesh['rows_0'=4,'rows_1'=4,'cols_0'=4,'cols_1'=4,'cols_2'=2] {'cols_1'}, use_global_device_ids=true, to_apply=%region_12.14 | all-reduce | flops 1 | bytes 8 | tf_op jit(solution)/shard_map/psum | solution.py:53
  232.1 3.1 psum.39
  235.9 0.6 fusion.31
  236.5 63.4 %reduce-scatter.5.cloned.1.call-done = bf16[1,256,128]{2,1,0:T(8,128)(2,1)} async-done(((bf16[16,256,128]{2,1,0:T(8,128)(2,1)}), bf16[1,256,128]{2,1,0:T(8,128)(2,1)}) %reduce-scatter.5.cloned.1.call-update) | async-done | bytes 65552 | tf_op jit(solution)/shard_map/reduce_scatter | solution.py:42
  299.9 1.5 multiply_subtract_fusion
  (57 shorter events, 6.1 us)
Async XLA Ops:
  9.6 22.9 %all-to-all-start = ((bf16[16,128,128]{2,1,0:T(8,128)(2,1)}), bf16[16,128,128]{2,1,0:T(8,128)(2,1)S(1)}, u32[]{:S(2)}, u32[]{:S(2)}) async-start(bf16[16,128,128]{2,1,0:T(8,128)(2,1)} %broadcast_in_dim.11), calls=%async_computation | async-start | bytes 1048576 | tf_op jit(solution)/shard_map/all_to_all | solution.py:16
  34.3 114.2 %all-to-all-start.1 = ((bf16[32,256,128]{2,1,0:T(8,128)(2,1)}), bf16[32,256,128]{2,1,0:T(8,128)(2,1)S(1)}, u32[]{:S(2)}, u32[]{:S(2)}) async-start(bf16[32,256,128]{2,1,0:T(8,128)(2,1)} %stack.5), calls=%async_computation.1 | async-start | bytes 4194304 | tf_op jit(solution)/shard_map/all_to_all | solution.py:131
  49.6 131.6 %reduce-scatter.3.cloned.1.call-start = ((), (), s32[]{:S(2)}) async-start(), calls=%async_computation.5 | async-start | bytes 3145728 | tf_op jit(solution)/shard_map/reduce_scatter | solution.py:41
  53.9 2.4 copy-start.15
  77.9 3.0 copy-start.18
  148.5 3.7 %copy-start.8 = (bf16[8,256,128]{2,1,0:T(8,128)(2,1)S(1)}, bf16[8,256,128]{2,1,0:T(8,128)(2,1)}, u32[]{:S(2)}) copy-start(bf16[8,256,128]{2,1,0:T(8,128)(2,1)} %gather_fusion.3) | copy-start | bytes 1572868
  148.5 4.2 %copy-start.11 = (s32[8,256,256]{1,2,0:T(8,128)S(1)}, s32[8,256,256]{1,2,0:T(8,128)}, u32[]{:S(2)}) copy-start(s32[8,256,256]{1,2,0:T(8,128)} %copy.27) | copy-start | bytes 6291460
  152.2 1.0 copy-start.7
  152.2 1.4 copy-start.14
  153.5 2.0 copy-start.10
  155.0 3.3 %copy-start = (bf16[8,256,256]{1,2,0:T(8,128)(2,1)}, bf16[8,256,256]{1,2,0:T(8,128)(2,1)S(1)}, u32[]{:S(2)}) copy-start(bf16[8,256,256]{1,2,0:T(8,128)(2,1)S(1)} %get-tuple-element.39) | copy-start | bytes 3145732
  155.0 1.4 copy-start.6
  155.0 1.8 copy-start.13
  156.8 2.1 copy-start.9
  158.3 3.3 %copy-start.2 = (bf16[8,256,256]{1,2,0:T(8,128)(2,1)}, bf16[8,256,256]{1,2,0:T(8,128)(2,1)S(1)}, u32[]{:S(2)}) copy-start(bf16[8,256,256]{1,2,0:T(8,128)(2,1)S(1)} %get-tuple-element.37) | copy-start | bytes 3145732
  158.3 1.4 copy-start.5
  158.3 1.8 copy-start.12
  161.6 1.0 copy-start.4
  164.3 1.9 copy-start.3
  164.4 2.2 copy-start.1
  172.5 63.4 %copy-start.17 = (f32[1,128,128]{2,1,0:T(8,128)S(1)}, f32[1,128,128]{2,1,0:T(8,128)}, u32[]{:S(2)}) copy-start(f32[1,128,128]{2,1,0:T(8,128)} %param.8) | copy-start | bytes 196612
  172.5 127.4 %copy-start.16 = (f32[1,256,128]{2,1,0:T(8,128)S(1)}, f32[1,256,128]{2,1,0:T(8,128)}, u32[]{:S(2)}) copy-start(f32[1,256,128]{2,1,0:T(8,128)} %param.7) | copy-start | bytes 393220
  173.6 62.2 %all-to-all-start.2 = ((bf16[16,128,128]{2,1,0:T(8,128)(2,1)}), bf16[16,128,128]{2,1,0:T(8,128)(2,1)S(1)}, u32[]{:S(2)}, u32[]{:S(2)}) async-start(bf16[16,128,128]{2,1,0:T(8,128)(2,1)} %convert_element_type.103), calls=%async_computation.4 | async-start | bytes 1048576 | tf_op jit(solution)/shard_map/all_to_all | solution.py:47
  181.1 118.8 %reduce-scatter.5.cloned.1.call-start = ((), (), s32[]{:S(2)}) async-start(), calls=%async_computation.6 | async-start | bytes 1114112 | tf_op jit(solution)/shard_map/reduce_scatter | solution.py:42
Sparse Core Ops, SparseCore 0:
  164.5 14.2 reduce-scatter.2
  186.0 113.9 reduce-scatter.4
